TPU v7x, 512 devices: a whole 4x8x8 slice. The times are simulated.
512 devices in a mesh: row: 16 (over z_lo, y), col: 32 (over x, z_hi, core).
Axes of the slice: x: 4, y: 8, z: 8 (z_hi: 4, z_lo: 2; z = z_hi * 2 + z_lo), core: 2. Of those that a mesh axis runs over, the one named last changes fastest.
Arguments:
- amplitudes: bfloat16 [4096, 262144], P(None, ('row', 'col')), may hold values from -6 to 6
- integrals: bfloat16 [256, 262144], P(None, ('row', 'col')), may hold values from -6 to 6
- hh_coupling: bfloat16 [256, 4096], P('row'), may hold values from -0.09375 to 0.09375
- thc_factor: bfloat16 [512, 1024], P(None, ('row', 'col')), may hold values from -0.25 to 0.25
- thc_core: float32 [1024, 1024], P('col', 'row'), may hold values from -3 to 3
- occ_energy: float32 [64], replicated, may hold values from -2 to -0.5
- vir_energy: float32 [512], replicated, may hold values from 0.3 to 3
- pair_owner: int32 [256], replicated, may hold values from 0 to 4095, as said below
Outputs:
- updated: bfloat16 [256, 262144], P(None, ('row', 'col'))
Inputs may be any that keep to these rules, and one draw needn't show every extreme that they name: pair_owner holds 256 distinct occupied pairs.
All inputs are finite; a program needn't handle non-finite values.
Results may differ from a plain program's by a relative error of at most 0.007.
Values may be sent and summed in bfloat16 or wider, within the bound.
A program may use at most 64 MiB of HBM per device.

v0:
```python
import jax
import jax.numpy as jnp
from jax import lax
from jax.sharding import Mesh
from jax.sharding import PartitionSpec as P

ROW = ("row_0", "row_1")
ROW_COL = ("row_0", "row_1", "col")


def in_order(pieces, dim):
    pieces = jnp.moveaxis(pieces, 0, dim)
    dims = pieces.shape
    return pieces.reshape(*dims[:dim], dims[dim] * dims[dim + 1], *dims[dim + 2 :])


def sent_to_all(shard, axis):
    count = lax.axis_size(axis)
    return lax.all_to_all(
        jnp.broadcast_to(shard[None], (count, *shard.shape)), axis, 0, 0, tiled=True
    )


def gather_directly(shard, axis, dim):
    return in_order(sent_to_all(shard, axis), dim)


def gather_in_order(shard, axes, order):
    pieces = shard[None]
    for k in order:
        pieces = lax.all_gather(pieces, axes[k], axis=0, tiled=True)
    carried = [lax.axis_size(axes[k]) for k in reversed(order)]
    pieces = pieces.reshape(*carried, *shard.shape)
    turned = sorted(range(len(order)), key=lambda place: order[len(order) - 1 - place])
    return pieces.transpose(*turned, *range(len(order), pieces.ndim)).reshape(-1, *shard.shape)


def gathered_by_axis(shard, axes, order, dim):
    return in_order(gather_in_order(shard, axes, order), dim)


def cut_along(shard, dim, count):
    dims = shard.shape
    pieces = shard.reshape(*dims[:dim], count, dims[dim] // count, *dims[dim + 1 :])
    return jnp.moveaxis(pieces, dim, 0)


def exchange_both(shard, axis, axes, splits, concats):
    sizes = [lax.axis_size(a) for a in axes]
    pieces = cut_along(shard, splits[0], sizes[0])
    pieces = jnp.moveaxis(cut_along(pieces, splits[1] + 1, sizes[1]), 0, 1)
    inside = pieces.shape[2:]
    pieces = pieces.reshape(-1, *inside)
    pieces = lax.all_to_all(pieces, axis, split_axis=0, concat_axis=0, tiled=True)
    pieces = in_order(pieces.reshape(*sizes, *inside), concats[0] + 1)
    return in_order(pieces, concats[1])


def per_device(
    amplitudes, integrals, hh_coupling, thc_factor, thc_core, occ_energy, vir_energy, pair_owner
):
    row_count = lax.axis_size(ROW)
    col_count = lax.axis_size("col")
    row_index = lax.axis_index(ROW)
    col_index = lax.axis_index("col")
    virtual = vir_energy.shape[0]
    column_width = amplitudes.shape[1]
    orb_block = column_width // virtual
    pairs_all = pair_owner.shape[0]
    pairs_col = pairs_all // col_count
    occupied = occ_energy.shape[0]
    factor = lax.all_gather(thc_factor, ROW_COL, axis=1, tiled=True)
    points = factor.shape[1]
    block_points = points // row_count
    core_block = gather_directly(thc_core, "col", 0)
    owned = amplitudes[pair_owner]
    coupled = jnp.dot(
        gathered_by_axis(hh_coupling, ROW, (0, 1), 0),
        amplitudes,
        preferred_element_type=jnp.float32,
    )
    local_half = jnp.einsum(
        "pkd,dq->pkq",
        owned.reshape(pairs_all, orb_block, virtual),
        factor,
        preferred_element_type=jnp.float32,
    ).astype(jnp.bfloat16)
    sectioned = local_half.reshape(col_count, pairs_col, 1, 1, orb_block, row_count, block_points)
    moved = exchange_both(sectioned, ROW_COL, (ROW, "col"), (5, 0), (2, 3))
    half = moved.reshape(pairs_col, virtual, block_points)
    middle = jnp.einsum("cP,pcq->pPq", factor, half, preferred_element_type=jnp.float32)
    weighted = (core_block[None] * middle).astype(jnp.bfloat16)
    back = jnp.einsum("aP,pPq->paq", factor, weighted, preferred_element_type=jnp.float32).astype(
        jnp.bfloat16
    )
    vir_slice = virtual // row_count
    sectioned_back = back.reshape(pairs_col, row_count, vir_slice, block_points)
    gathered_back = lax.all_to_all(sectioned_back, ROW, split_axis=1, concat_axis=3, tiled=True)
    gathered_back = gathered_back.reshape(pairs_col, vir_slice, row_count, block_points)
    factor_split = factor.reshape(virtual, row_count, block_points)
    partial_value = jnp.einsum(
        "parq,brq->rapb", gathered_back, factor_split, preferred_element_type=jnp.float32
    ).astype(jnp.bfloat16)
    ladder = jnp.sum(partial_value.astype(jnp.float32), axis=0).astype(jnp.bfloat16)
    ladder = ladder.reshape(col_count, orb_block, pairs_col, virtual)
    returned = lax.all_to_all(ladder, "col", split_axis=0, concat_axis=2, tiled=True)
    returned = (
        returned.reshape(orb_block, pairs_all, virtual)
        .transpose(1, 0, 2)
        .reshape(pairs_all, column_width)
    )
    device = row_index * col_count + col_index
    vir_mine = lax.dynamic_slice_in_dim(vir_energy, device * orb_block, orb_block, 0)
    orbital_ids = jnp.arange(occupied, dtype=jnp.int32)
    first_hit = (pair_owner // occupied)[:, None] == orbital_ids[None, :]
    second_hit = (pair_owner % occupied)[:, None] == orbital_ids[None, :]
    first_occ = jnp.sum(jnp.where(first_hit, occ_energy[None, :], 0.0), axis=1)
    second_occ = jnp.sum(jnp.where(second_hit, occ_energy[None, :], 0.0), axis=1)
    vir_pairs = vir_mine[:, None] + vir_energy[None, :]
    denom = vir_pairs - (first_occ + second_occ)[:, None]
    rest = integrals.astype(jnp.float32) + coupled + returned.astype(jnp.float32)
    update = 0.4 * owned.astype(jnp.float32) + 0.6 * rest / denom
    return update.astype(jnp.bfloat16)


def solution(mesh):
    finer = Mesh(mesh.devices.reshape(2, 8, mesh.shape["col"]), ("row_0", "row_1", "col"))
    in_specs = (
        P(None, ROW_COL),
        P(None, ROW_COL),
        P(ROW, None),
        P(None, ROW_COL),
        P("col", ROW),
        P(),
        P(),
        P(),
    )
    out_specs = P(None, ROW_COL)
    return jax.shard_map(
        per_device, mesh=finer, in_specs=in_specs, out_specs=out_specs, check_vma=False
    )
```

profile of v0, /device:TPU:1, one launch (start us, length us, event | category | flops | bytes accessed | tf_op | source)
XLA Modules:
  0.0 883.5 jit_solution(17219511499074198008)
XLA Ops:
  6.5 0.0 all-gather.7.cloned.1.call-start
  6.5 0.7 all-gather.7.cloned.1.call-update
  7.3 0.8 broadcast_in_dim.39
  8.0 1.0 reshape.74
  9.1 14.5 %all-to-all-start = ((f32[32,1,2048]{2,1,0:T(1,128)}), f32[32,1,2048]{2,1,0:T(1,128)}, u32[]{:S(2)}, u32[]{:S(2)}) async-start(f32[32,1,2048]{2,1,0:T(1,128)} %reshape.74), calls=%async_computation | async-start | bytes 524288 | tf_op jit(solution)/shard_map/all_to_all | solution.py:19
  23.5 0.0 all-gather.5.cloned.1.call-start
  23.6 10.7 %all-gather = bf16[32,4096]{1,0:T(8,128)(2,1)} all-gather(bf16[16,4096]{1,0:T(8,128)(2,1)} %param.10), channel_id=2, replica_groups=mesh['row_0'=2,'row_1'=8,'col'=32] {'row_0'}, dimensions={0}, use_global_device_ids=true | all-gather | bytes 393216 | tf_op jit(solution)/shard_map/all_gather | solution.py:31
  34.3 0.0 all-gather.5.cloned.1.call-update
  34.3 0.0 copy-done.3
  34.4 3.9 gather_fusion
  38.3 741.5 %all-gather.7.cloned.1.call-done = bf16[512,2,512]{2,1,0:T(2,128)(2,1)} async-done(((bf16[1,2,512]{2,1,0:T(2,128)(2,1)}), bf16[512,2,512]{2,1,0:T(2,128)(2,1)}) %all-gather.7.cloned.1.call-update) | async-done | bytes 1048592 | tf_op jit(solution)/shard_map/all_gather | solution.py:72
  779.8 1.5 reshape.68
  781.3 0.5 convolution_convert_fusion
  781.8 0.7 reshape_reshape.13
  782.4 0.3 copy.39
  782.7 0.0 copy-start
  782.7 1.4 reshape.72
  784.2 0.0 all-to-all-done
  784.2 12.4 %all-to-all-start.1 = ((bf16[512,2,256]{2,1,0:T(2,128)(2,1)}), bf16[512,2,256]{2,1,0:T(2,128)(2,1)S(1)}, u32[]{:S(2)}, u32[]{:S(2)}) async-start(bf16[512,2,256]{2,1,0:T(2,128)(2,1)} %reshape.72), calls=%async_computation.1 | async-start | bytes 1048576 | tf_op jit(solution)/shard_map/all_to_all | solution.py:54
  796.6 0.5 broadcast.20
  797.1 2.9 reduce.2
  800.0 1.1 reshape.75
  801.2 0.9 copy.38
  802.1 0.0 copy-done
  802.1 1.2 reshape.69
  803.3 20.9 %all-to-all-done.1 = bf16[512,2,256]{2,1,0:T(2,128)(2,1)S(1)} async-done(((bf16[512,2,256]{2,1,0:T(2,128)(2,1)}), bf16[512,2,256]{2,1,0:T(2,128)(2,1)S(1)}, u32[]{:S(2)}, u32[]{:S(2)}) %all-to-all-start.1) | async-done | bytes 524320 | tf_op jit(solution)/shard_map/all_to_all | solution.py:54
  824.2 0.6 reshape.73
  824.8 1.0 bitcast_bitcast_fusion
  825.9 0.5 copy-done.1
  826.4 4.2 fusion.1
  830.6 1.5 copy.43
  832.1 0.1 copy.55
  832.2 0.7 reshape.76
  833.0 15.6 %all_to_all.34 = bf16[16,2,8192]{2,1,0:T(2,128)(2,1)S(1)} all-to-all(bf16[16,2,8192]{2,1,0:T(2,128)(2,1)S(1)} %reshape.76), channel_id=1, replica_groups=mesh['row_0'=2,'row_1'=8,'col'=32] {'row_0','row_1'}, dimensions={0} | all-to-all | bytes 1048576 | tf_op jit(solution)/shard_map/all_to_all | solution.py:98
  848.5 0.7 reshape.77
  849.2 0.0 copy-start.2
  849.2 0.0 copy-start.4
  849.2 1.2 convert_reduce_fusion
  850.4 0.9 copy.45
  851.3 7.9 all-to-all-start.3
  859.2 0.7 dynamic_slice.3
  859.9 0.1 select_reduce_fusion
  860.0 0.6 broadcast_add_fusion
  860.6 0.0 all-gather.5.cloned.1.call-done
  860.7 0.0 copy-start.5
  860.7 1.8 copy.37
  862.4 10.0 %all-to-all-done.3 = bf16[32,1,8,512]{3,2,1,0:T(8,128)(2,1)S(1)} async-done(((bf16[32,1,8,512]{3,2,1,0:T(8,128)(2,1)}), bf16[32,1,8,512]{3,2,1,0:T(8,128)(2,1)S(1)}, u32[]{:S(2)}, u32[]{:S(2)}) %all-to-all-start.3) | async-done | bytes 262176 | tf_op jit(solution)/shard_map/all_to_all | solution.py:106
  872.5 4.2 fusion.6
  (8 shorter events, 0.0 us)
Async XLA Ops:
  6.5 27.8 %copy-start.3 = (s32[256]{0:T(256)S(1)}, s32[256]{0:T(256)}, u32[]{:S(2)}) copy-start(s32[256]{0:T(256)} %param.15) | copy-start | bytes 3076
  6.5 773.3 %all-gather.7.cloned.1.call-start = ((), (), s32[]{:S(2)}) async-start(), calls=%async_computation.5 | async-start | bytes 1050624 | tf_op jit(solution)/shard_map/all_gather | solution.py:72
  9.1 775.1 %all-to-all-start = ((f32[32,1,2048]{2,1,0:T(1,128)}), f32[32,1,2048]{2,1,0:T(1,128)}, u32[]{:S(2)}, u32[]{:S(2)}) async-start(f32[32,1,2048]{2,1,0:T(1,128)} %reshape.74), calls=%async_computation | async-start | bytes 524288 | tf_op jit(solution)/shard_map/all_to_all | solution.py:19
  23.5 837.1 %all-gather.5.cloned.1.call-start = ((), (), s32[]{:S(2)}) async-start(), calls=%async_computation.4 | async-start | bytes 2359296 | tf_op jit(solution)/shard_map/all_gather | solution.py:31
  782.7 19.4 %copy-start = (bf16[512,2,512]{2,1,0:T(2,128)(2,1)S(1)}, bf16[512,2,512]{2,1,0:T(2,128)(2,1)}, u32[]{:S(2)}) copy-start(bf16[512,2,512]{2,1,0:T(2,128)(2,1)} %all-gather.7.cloned.1.call-done) | copy-start | bytes 3145732
  784.2 40.0 %all-to-all-start.1 = ((bf16[512,2,256]{2,1,0:T(2,128)(2,1)}), bf16[512,2,256]{2,1,0:T(2,128)(2,1)S(1)}, u32[]{:S(2)}, u32[]{:S(2)}) async-start(bf16[512,2,256]{2,1,0:T(2,128)(2,1)} %reshape.72), calls=%async_computation.1 | async-start | bytes 1048576 | tf_op jit(solution)/shard_map/all_to_all | solution.py:54
  824.8 1.6 copy-start.1
  849.2 10.0 %copy-start.2 = (f32[512]{0:T(512)S(1)}, f32[512]{0:T(512)}, u32[]{:S(2)}) copy-start(f32[512]{0:T(512)} %param.14) | copy-start | bytes 6148
  849.2 10.7 %copy-start.4 = (f32[64]{0:T(128)S(1)}, f32[64]{0:T(128)}, u32[]{:S(2)}) copy-start(f32[64]{0:T(128)} %param.13) | copy-start | bytes 772
  851.3 21.2 %all-to-all-start.3 = ((bf16[32,1,8,512]{3,2,1,0:T(8,128)(2,1)}), bf16[32,1,8,512]{3,2,1,0:T(8,128)(2,1)S(1)}, u32[]{:S(2)}, u32[]{:S(2)}) async-start(bf16[32,1,8,512]{3,2,1,0:T(8,128)(2,1)} %copy.45), calls=%async_computation.3 | async-start | bytes 524288 | tf_op jit(solution)/shard_map/all_to_all | solution.py:106
  860.7 11.8 %copy-start.5 = (bf16[256,512]{1,0:T(8,128)(2,1)S(1)}, bf16[256,512]{1,0:T(8,128)(2,1)}, u32[]{:S(2)}) copy-start(bf16[256,512]{1,0:T(8,128)(2,1)} %param.9) | copy-start | bytes 786436
Sparse Core Ops, SparseCore 0:
  9.5 770.3 all-gather.6
  781.9 45.5 all-gather.4
where the time goes:
time: 884 us
  waiting for transfers between devices  773 us (87%)
  starting transfers between devices  34.8 us (4%)
  blocking collectives  26.3 us (3%)
  local copies, waits for them, and re-layouts  21.9 us (2%)
  between operations  13.6 us (2%)
  matrix products  10.1 us (1%)
    all_gather x1, waiting for transfers between devices, per_device(): factor = lax.all_gather(thc_factor, ROW_COL, axis=1, tiled=True)  742 us
    all_to_all x1, waiting for transfers between devices, exchange_both(): lax.all_to_all(pieces, axis, split_axis=0, concat_axis=0, tiled=True)  20.9 us
  transfers between devices with their start and end apart: 5, of which 3 were waited for; matrix products, arithmetic and copies ran while one was open for 3% of the time, Pallas kernels for 0%

commit v1 on v0

--- a/solution.py
+++ b/solution.py
@@ -69,7 +69,9 @@
     pairs_all = pair_owner.shape[0]
     pairs_col = pairs_all // col_count
     occupied = occ_energy.shape[0]
-    factor = lax.all_gather(thc_factor, ROW_COL, axis=1, tiled=True)
+    factor = jnp.concatenate(
+        lax.all_to_all(jnp.stack([thc_factor] * lax.axis_size(ROW_COL)), ROW_COL, 0, 0), axis=1
+    )
     points = factor.shape[1]
     block_points = points // row_count
     core_block = gather_directly(thc_core, "col", 0)

time: 884 us -> 181 us (0.20)
  waiting for transfers between devices: 773 us -> 47.5 us
  starting transfers between devices: 34.8 us -> 55.3 us
    all_gather x1 -> x0, waiting for transfers between devices: 742 us -> none  [per_device(): factor = lax.all_gather(thc_factor, ROW_COL, axis=1, tiled=True)]
    all_to_all x0 -> x2, starting transfers between devices: none -> 25.8 us  [the longest x1 22.1 us: per_device(): lax.all_to_all(jnp.stack([thc_factor] * lax.axis_size(ROW_COL)), ROW_COL,...]
    all_to_all x0 -> x2, waiting for transfers between devices: none -> 18.9 us  [the longest x1 12.5 us: per_device(): lax.all_to_all(sectioned_back, ROW, split_axis=1, concat_axis=3, tiled=True)]
    all_to_all x1 -> x0, blocking collectives: 15.6 us -> none  [per_device(): lax.all_to_all(sectioned_back, ROW, split_axis=1, concat_axis=3, tiled=True)]
    all_gather x1, blocking collectives: 10.7 us -> 25.4 us  [gather_in_order(): pieces = lax.all_gather(pieces, axes[k], axis=0, tiled=True)]
    all_to_all x1, starting transfers between devices: 14.5 us -> 4.96 us  [sent_to_all(): lax.all_to_all(jnp.broadcast_to(shard[None], (count, *shard.shape)), axis...]
  transfers between devices with their start and end apart: 5 -> 6, of which waited for: 3 -> 5; matrix products, arithmetic and copies ran while one was open for 3% -> 18% of each run, Pallas kernels for 0% -> 0%
where the time goes in v1:
time: 181 us; the launch traced here: 180 us
  starting transfers between devices  55.3 us (31%)
  waiting for transfers between devices  47.5 us (26%)
  blocking collectives  25.4 us (14%)
  local copies, waits for them, and re-layouts  25.1 us (14%)
  between operations  13.6 us (8%)
  matrix products  10.1 us (6%)
  other arithmetic  2.96 us (2%)
    all_gather x1, blocking collectives, gather_in_order(): pieces = lax.all_gather(pieces, axes[k], axis=0, tiled=True)  25.4 us
    all_to_all x1, starting transfers between devices, per_device(): lax.all_to_all(jnp.stack([thc_factor] * lax.axis_size(ROW_COL)), ROW_COL,...  22.1 us
    all_to_all x1, starting transfers between devices, exchange_both(): lax.all_to_all(pieces, axis, split_axis=0, concat_axis=0, tiled=True)  16.6 us
    all_to_all x1, waiting for transfers between devices, exchange_both(): lax.all_to_all(pieces, axis, split_axis=0, concat_axis=0, tiled=True)  16.6 us
    all_to_all x1, waiting for transfers between devices, per_device(): lax.all_to_all(sectioned_back, ROW, split_axis=1, concat_axis=3, tiled=True)  12.5 us
    all_to_all x1, waiting for transfers between devices, per_device(): lax.all_to_all(ladder, 'col', split_axis=0, concat_axis=2, tiled=True)  10.1 us
    unnamed x18, local copies, waits for them, and re-layouts  8.65 us
    all_to_all x1, starting transfers between devices, per_device(): lax.all_to_all(ladder, 'col', split_axis=0, concat_axis=2, tiled=True)  7.91 us
  transfers between devices with their start and end apart: 6, of which 5 were waited for; matrix products, arithmetic and copies ran while one was open for 18% of the time, Pallas kernels for 0%

profile of v1, /device:TPU:1, one launch (start us, length us, event | category | flops | bytes accessed | tf_op | source)
XLA Modules:
  0.0 179.9 jit_solution(14006782499568503142)
XLA Ops:
  6.5 2.2 %stack.2 = bf16[512,512,2]{1,2,0:T(2,128)(2,1)} broadcast(bf16[512,2]{0,1:T(2,128)(2,1)} %param.11), dimensions={1,2} | broadcast | bytes 1050624 | tf_op jit(solution)/shard_map/stack | solution.py:73
  8.8 22.1 %all-to-all-start.1 = ((bf16[512,512,2]{1,2,0:T(2,128)(2,1)}), bf16[512,512,2]{1,2,0:T(2,128)(2,1)S(1)}, u32[]{:S(2)}, u32[]{:S(2)}) async-start(bf16[512,512,2]{1,2,0:T(2,128)(2,1)} %stack.2), calls=%async_computation.1 | async-start | bytes 2097152 | tf_op jit(solution)/shard_map/all_to_all | solution.py:73
  30.9 0.0 all-gather.3.cloned.1.call-start
  31.0 0.0 copy-done
  31.0 25.4 %all-gather = bf16[32,4096]{1,0:T(8,128)(2,1)} all-gather(bf16[16,4096]{1,0:T(8,128)(2,1)S(1)} %copy-done), channel_id=2, replica_groups=mesh['row_0'=2,'row_1'=8,'col'=32] {'row_0'}, dimensions={0}, use_global_device_ids=true | all-gather | bytes 393216 | tf_op jit(solution)/shard_map/all_gather | solution.py:31
  56.4 0.0 all-gather.3.cloned.1.call-update
  56.4 0.0 copy-done.1
  56.4 0.1 broadcast_in_dim.39
  56.5 1.0 reshape.79
  57.5 6.4 %all-to-all-done.1 = bf16[512,512,2]{1,2,0:T(2,128)(2,1)S(1)} async-done(((bf16[512,512,2]{1,2,0:T(2,128)(2,1)}), bf16[512,512,2]{1,2,0:T(2,128)(2,1)S(1)}, u32[]{:S(2)}, u32[]{:S(2)}) %all-to-all-start.1) | async-done | bytes 1048608 | tf_op jit(solution)/shard_map/all_to_all | solution.py:73
  64.0 5.0 %all-to-all-start = ((f32[32,1,2048]{2,1,0:T(1,128)}), f32[32,1,2048]{2,1,0:T(1,128)}, u32[]{:S(2)}, u32[]{:S(2)}) async-start(f32[32,1,2048]{2,1,0:T(1,128)} %reshape.79), calls=%async_computation | async-start | bytes 524288 | tf_op jit(solution)/shard_map/all_to_all | solution.py:19
  69.0 3.9 %gather_fusion = bf16[256,512]{1,0:T(8,128)(2,1)S(1)} fusion(bf16[4096,512]{1,0:T(8,128)(2,1)} %param.8, s32[1024]{0:T(1024)S(1)} %pad_clamp_fusion), kind=kCustom, calls=%fused_computation | custom fusion | bytes 525312 | tf_op jit(solution)/shard_map/gather | solution.py:78
  72.9 0.4 reshape.56
  73.4 1.3 convolution_convert_fusion
  74.6 1.8 reshape_reshape.16
  76.4 1.3 copy.48
  77.7 3.0 %reshape.77 = bf16[512,2,256]{2,1,0:T(2,128)(2,1)} reshape(bf16[512,1,1,1,1,1,8,64]{7,6,5,4,3,2,1,0:T(8,128)(2,1)} %bitcast.74) | data formatting | bytes 1048576
  80.6 1.8 %all-to-all-done = f32[32,1,2048]{2,1,0:T(1,128)} async-done(((f32[32,1,2048]{2,1,0:T(1,128)}), f32[32,1,2048]{2,1,0:T(1,128)}, u32[]{:S(2)}, u32[]{:S(2)}) %all-to-all-start) | async-done | bytes 262176 | tf_op jit(solution)/shard_map/all_to_all | solution.py:19
  82.4 16.6 %all-to-all-start.2 = ((bf16[512,2,256]{2,1,0:T(2,128)(2,1)}), bf16[512,2,256]{2,1,0:T(2,128)(2,1)}, u32[]{:S(2)}, u32[]{:S(2)}) async-start(bf16[512,2,256]{2,1,0:T(2,128)(2,1)} %reshape.77), calls=%async_computation.2 | async-start | bytes 1048576 | tf_op jit(solution)/shard_map/all_to_all | solution.py:54
  99.1 0.5 broadcast.22
  99.6 2.2 %reduce.2 = f32[32,2048]{1,0:T(8,128)S(1)} reduce(f32[32,1,2048]{2,1,0:T(1,128)} %all-to-all-done, f32[]{:T(128)} %broadcast.22), dimensions={1}, to_apply=%all_to_all.27.reduce_sub_computation | reduce | bytes 524292 | tf_op jit(solution)/shard_map/all_to_all | solution.py:19
  101.8 0.2 reshape.80
  102.0 0.9 copy.47
  102.9 16.6 %all-to-all-done.2 = bf16[512,2,256]{2,1,0:T(2,128)(2,1)} async-done(((bf16[512,2,256]{2,1,0:T(2,128)(2,1)}), bf16[512,2,256]{2,1,0:T(2,128)(2,1)}, u32[]{:S(2)}, u32[]{:S(2)}) %all-to-all-start.2) | async-done | bytes 524320 | tf_op jit(solution)/shard_map/all_to_all | solution.py:54
  119.5 2.2 %reshape.78 = bf16[512,1,1,1,1,1,8,64]{7,6,5,4,3,2,1,0:T(8,128)(2,1)S(1)} reshape(bf16[512,2,256]{2,1,0:T(2,128)(2,1)} %all-to-all-done.2) | data formatting | bytes 1048576
  121.8 1.0 bitcast_bitcast_fusion
  122.8 3.4 %fusion.1 = bf16[8,512,64]{1,2,0:T(8,128)(2,1)S(1)} fusion(bf16[512,1024]{0,1:T(8,128)(2,1)S(1)} %reshape.56, bf16[8,512,64]{2,0,1:T(8,128)(2,1)} %bitcast_bitcast_fusion, f32[1024,64]{0,1:T(8,128)} %copy.47), kind=kOutput, calls=%fused_computation.6 | convolution fusion | flops 1075052544 | bytes 2359296 | tf_op jit(solution)/shard_map/aP,pPq->paq/dot_general | solution.py:95
  126.2 0.5 copy.54
  126.7 0.1 copy.70
  126.8 1.5 reshape.81
  128.3 3.6 %all-to-all-start.3 = ((bf16[16,2,8192]{2,1,0:T(2,128)(2,1)}), bf16[16,2,8192]{2,1,0:T(2,128)(2,1)S(1)}, u32[]{:S(2)}, u32[]{:S(2)}) async-start(bf16[16,2,8192]{2,1,0:T(2,128)(2,1)} %reshape.81), calls=%async_computation.3 | async-start | bytes 1048576 | tf_op jit(solution)/shard_map/all_to_all | solution.py:100
  131.9 0.4 reshape.75
  132.4 12.5 %all-to-all-done.3 = bf16[16,2,8192]{2,1,0:T(2,128)(2,1)S(1)} async-done(((bf16[16,2,8192]{2,1,0:T(2,128)(2,1)}), bf16[16,2,8192]{2,1,0:T(2,128)(2,1)S(1)}, u32[]{:S(2)}, u32[]{:S(2)}) %all-to-all-start.3) | async-done | bytes 524320 | tf_op jit(solution)/shard_map/all_to_all | solution.py:100
  144.8 0.7 reshape.82
  145.5 0.0 copy-start.2
  145.5 0.0 copy-start.4
  145.5 1.2 convert_reduce_fusion
  146.7 0.9 copy.56
  147.6 7.9 %all-to-all-start.4 = ((bf16[32,1,8,512]{3,2,1,0:T(8,128)(2,1)}), bf16[32,1,8,512]{3,2,1,0:T(8,128)(2,1)S(1)}, u32[]{:S(2)}, u32[]{:S(2)}) async-start(bf16[32,1,8,512]{3,2,1,0:T(8,128)(2,1)} %copy.56), calls=%async_computation.4 | async-start | bytes 524288 | tf_op jit(solution)/shard_map/all_to_all | solution.py:108
  155.5 0.6 dynamic_slice.3
  156.2 0.0 copy-done.4
  156.2 0.1 select_reduce_fusion
  156.3 0.6 broadcast_add_fusion
  156.9 0.0 all-gather.3.cloned.1.call-done
  156.9 0.0 copy-start.5
  157.0 1.8 copy.46
  158.7 10.1 %all-to-all-done.4 = bf16[32,1,8,512]{3,2,1,0:T(8,128)(2,1)S(1)} async-done(((bf16[32,1,8,512]{3,2,1,0:T(8,128)(2,1)}), bf16[32,1,8,512]{3,2,1,0:T(8,128)(2,1)S(1)}, u32[]{:S(2)}, u32[]{:S(2)}) %all-to-all-start.4) | async-done | bytes 262176 | tf_op jit(solution)/shard_map/all_to_all | solution.py:108
  168.8 4.2 %fusion.6 = bf16[256,512]{1,0:T(8,128)(2,1)} fusion(bf16[256,4096]{1,0:T(8,128)(2,1)S(1)} %bitcast.79, bf16[4096,512]{1,0:T(8,128)(2,1)} %param.8, bf16[256,512]{1,0:T(8,128)(2,1)S(1)} %copy-done.5, bf16[256,512]{1,0:T(8,128)(2,1)S(1)} %gather_fusion, bf16[32,1,8,512]{3,2,1,0:T(8,128)(2,1)S(1)} %all-to-all-done.4, f32[256]{0:T(256)S(1)} %add.60, ...), kind=kOutput, calls=%fused_computation.12 | convolution fusion | flops 1075183616 | bytes 7343104 | tf_op jit(solution)/shard_map/dot_general | solution.py:79
  (9 shorter events, 0.0 us)
Async XLA Ops:
  6.5 24.5 %copy-start = (bf16[16,4096]{1,0:T(8,128)(2,1)S(1)}, bf16[16,4096]{1,0:T(8,128)(2,1)}, u32[]{:S(2)}) copy-start(bf16[16,4096]{1,0:T(8,128)(2,1)} %param.10) | copy-start | bytes 393220
  6.5 49.9 %copy-start.1 = (f32[32,64]{1,0:T(8,128)S(1)}, f32[32,64]{1,0:T(8,128)}, u32[]{:S(2)}) copy-start(f32[32,64]{1,0:T(8,128)} %param.12) | copy-start | bytes 24580
  8.8 60.2 %copy-start.3 = (s32[256]{0:T(256)S(1)}, s32[256]{0:T(256)}, u32[]{:S(2)}) copy-start(s32[256]{0:T(256)} %param.15) | copy-start | bytes 3076
  8.8 55.2 %all-to-all-start.1 = ((bf16[512,512,2]{1,2,0:T(2,128)(2,1)}), bf16[512,512,2]{1,2,0:T(2,128)(2,1)S(1)}, u32[]{:S(2)}, u32[]{:S(2)}) async-start(bf16[512,512,2]{1,2,0:T(2,128)(2,1)} %stack.2), calls=%async_computation.1 | async-start | bytes 2097152 | tf_op jit(solution)/shard_map/all_to_all | solution.py:73
  30.9 126.0 %all-gather.3.cloned.1.call-start = ((), (), s32[]{:S(2)}) async-start(), calls=%async_computation.5 | async-start | bytes 2359296 | tf_op jit(solution)/shard_map/all_gather | solution.py:31
  64.0 18.5 %all-to-all-start = ((f32[32,1,2048]{2,1,0:T(1,128)}), f32[32,1,2048]{2,1,0:T(1,128)}, u32[]{:S(2)}, u32[]{:S(2)}) async-start(f32[32,1,2048]{2,1,0:T(1,128)} %reshape.79), calls=%async_computation | async-start | bytes 524288 | tf_op jit(solution)/shard_map/all_to_all | solution.py:19
  82.4 37.1 %all-to-all-start.2 = ((bf16[512,2,256]{2,1,0:T(2,128)(2,1)}), bf16[512,2,256]{2,1,0:T(2,128)(2,1)}, u32[]{:S(2)}, u32[]{:S(2)}) async-start(bf16[512,2,256]{2,1,0:T(2,128)(2,1)} %reshape.77), calls=%async_computation.2 | async-start | bytes 1048576 | tf_op jit(solution)/shard_map/all_to_all | solution.py:54
  128.3 16.5 %all-to-all-start.3 = ((bf16[16,2,8192]{2,1,0:T(2,128)(2,1)}), bf16[16,2,8192]{2,1,0:T(2,128)(2,1)S(1)}, u32[]{:S(2)}, u32[]{:S(2)}) async-start(bf16[16,2,8192]{2,1,0:T(2,128)(2,1)} %reshape.81), calls=%async_computation.3 | async-start | bytes 1048576 | tf_op jit(solution)/shard_map/all_to_all | solution.py:100
  145.5 10.0 %copy-start.2 = (f32[512]{0:T(512)S(1)}, f32[512]{0:T(512)}, u32[]{:S(2)}) copy-start(f32[512]{0:T(512)} %param.14) | copy-start | bytes 6148
  145.5 10.7 %copy-start.4 = (f32[64]{0:T(128)S(1)}, f32[64]{0:T(128)}, u32[]{:S(2)}) copy-start(f32[64]{0:T(128)} %param.13) | copy-start | bytes 772
  147.6 21.2 %all-to-all-start.4 = ((bf16[32,1,8,512]{3,2,1,0:T(8,128)(2,1)}), bf16[32,1,8,512]{3,2,1,0:T(8,128)(2,1)S(1)}, u32[]{:S(2)}, u32[]{:S(2)}) async-start(bf16[32,1,8,512]{3,2,1,0:T(8,128)(2,1)} %copy.56), calls=%async_computation.4 | async-start | bytes 524288 | tf_op jit(solution)/shard_map/all_to_all | solution.py:108
  156.9 11.9 %copy-start.5 = (bf16[256,512]{1,0:T(8,128)(2,1)S(1)}, bf16[256,512]{1,0:T(8,128)(2,1)}, u32[]{:S(2)}) copy-start(bf16[256,512]{1,0:T(8,128)(2,1)} %param.9) | copy-start | bytes 786436
Sparse Core Ops, SparseCore 0:
  56.6 40.8 all-gather.2
